TPU v7x, 32 devices: a whole 2x2x4 slice. The times are simulated.
32 devices in a mesh: seq: 8 (over z, x), head: 4 (over y, core).
Axes of the slice: x: 2, y: 2, z: 4, core: 2. Of those that a mesh axis runs over, the one named last changes fastest.
Arguments:
- inputs: bfloat16 [8192, 4096], P('seq', 'head'), may hold values from -6 to 6
- out_grad: bfloat16 [8192, 4096], P('seq', 'head'), may hold values from -6 to 6
- b_proj: bfloat16 [8192, 128], P('seq'), may hold values from -0.75 to 0.75
- c_proj: bfloat16 [8192, 128], P('seq'), may hold values from -3 to 3
- step_raw: float32 [8192, 64], P('seq', 'head'), may hold values from -3 to 12
- log_rate: float32 [64], P('head'), may hold values from -7 to -1.7
- step_bias: float32 [64], P('head'), may hold values from -7 to -1.6
- skip_gain: float32 [64], P('head'), may hold values from 0.5 to 1.5
- saved_states: float32 [8, 64, 64, 128], P(None, 'seq', 'head'), may hold values from -1.5 to 1.5
- segment_slot: int32 [8], replicated, may hold values from 0 to 7, each once
Outputs:
- grad_inputs: bfloat16 [8192, 4096], P('seq', 'head')
- grad_step_raw: float32 [8192, 64], P('seq', 'head')
- grad_b: float32 [8192, 128], P(('seq', 'head'))
- grad_c: float32 [8192, 128], P(('seq', 'head'))
Inputs may be any that keep to these rules, and one draw needn't show every extreme that they name: `segment_slot`: a permutation of the segments.
All inputs are finite; a program needn't handle non-finite values.
Results may differ from a plain program's by a relative error of at most 0.0012.
Values sent between devices are 32-bit elements; how exact they have to be, the bound alone decides.
A program may use at most 128 MiB of HBM per device.

v0:
```python
import jax
import jax.numpy as jnp
from jax import lax
from jax.sharding import PartitionSpec as P

SPAN = 256


highest = lax.Precision.HIGHEST


def carried_in(value, axis, join, neutral):
    count, mine = (lax.axis_size(axis), lax.axis_index(axis))
    pieces = jax.tree.map(lambda part: lax.all_gather(part, axis), value)
    pieces = jax.tree.map(lambda part: part[::-1], pieces)
    mine = count - 1 - mine
    so_far = jax.tree.map(
        lambda part, zero: jnp.full_like(part, 0) + jnp.asarray(zero, part.dtype), value, neutral
    )

    def turn(position, so_far):
        longer = join(so_far, jax.tree.map(lambda part: part[position], pieces))
        return jax.tree.map(lambda new, old: jnp.where(position < mine, new, old), longer, so_far)

    return lax.fori_loop(0, count - 1, turn, so_far)


def carry_combine(earlier, later):
    return (later[0] * earlier[0], later[0][:, None, None] * earlier[1] + later[1])


def advance(carried, item):
    return (item[0][:, None, None] * carried + item[1], carried)


def on_device(
    inputs,
    out_grad,
    b_proj,
    c_proj,
    step_raw,
    log_rate,
    step_bias,
    skip_gain,
    saved_states,
    segment_slot,
):
    tok_rows = inputs.shape[0]
    head_count = step_raw.shape[1]
    state_dim = b_proj.shape[1]
    head_width = inputs.shape[1] // head_count
    block_count = tok_rows // SPAN
    seg_count = saved_states.shape[0]
    inverse_order = (
        jnp.zeros((seg_count,), jnp.int32)
        .at[segment_slot]
        .set(jnp.arange(seg_count, dtype=jnp.int32))
    )
    ordered = jnp.take(saved_states, inverse_order, axis=0)
    start_state = lax.all_to_all(
        lax.all_to_all(ordered, "seq", split_axis=0, concat_axis=1, tiled=True),
        "head",
        split_axis=1,
        concat_axis=2,
        tiled=True,
    )[0]
    shifted_raw = step_raw + step_bias[None, :]
    step_size = jax.nn.softplus(shifted_raw)
    decay_rate = jnp.exp(log_rate)
    log_decay = (-decay_rate[None, :] * step_size).reshape(block_count, SPAN, head_count)
    positions = jnp.arange(SPAN)
    lower_mask = positions[:, None] >= positions[None, :]
    cumulative = jnp.cumsum(log_decay, axis=1)
    block_end = cumulative[:, -1, :]
    step_blocks = step_size.reshape(block_count, SPAN, head_count)
    raw_blocks = shifted_raw.reshape(block_count, SPAN, head_count)
    input_blocks = inputs.reshape(block_count, SPAN, head_count, head_width)
    grad_blocks = out_grad.reshape(block_count, SPAN, head_count, head_width)
    b_blocks = b_proj.reshape(block_count, SPAN, state_dim)
    c_blocks = c_proj.reshape(block_count, SPAN, state_dim)
    to_end = jnp.exp(block_end[:, None, :] - cumulative)
    from_start = jnp.exp(cumulative)
    forward_part = jnp.einsum(
        "cuhp,cun->chpn",
        input_blocks.astype(jnp.float32) * (to_end * step_blocks)[..., None],
        b_blocks.astype(jnp.float32),
        precision=highest,
    )
    backward_part = jnp.einsum(
        "cvhp,cvn->chpn",
        grad_blocks.astype(jnp.float32) * from_start[..., None],
        c_blocks.astype(jnp.float32),
        precision=highest,
    )
    block_decay = jnp.exp(block_end)
    unused_end, entering = lax.scan(advance, start_state, (block_decay, forward_part))
    before = jnp.exp(jnp.cumsum(block_end, axis=0) - block_end)
    device_sum = jnp.einsum("ch,chpn->hpn", before, backward_part, precision=highest)
    device_decay = jnp.exp(jnp.sum(block_end, axis=0))
    identity = (jnp.ones_like(device_decay), jnp.zeros_like(device_sum))
    from_right = carried_in((device_decay, device_sum), "seq", carry_combine, identity)[1]
    unused_start, leaving = lax.scan(
        advance, from_right, (block_decay, backward_part), reverse=True
    )

    def one_block(unused_carry, item):
        (
            input_block,
            grad_block,
            b_block,
            c_block,
            step_block,
            raw_block,
            cumul_block,
            state_in,
            state_out,
        ) = item
        end_value = cumul_block[-1]
        intersection = jnp.einsum("vn,un->vu", c_block, b_block, preferred_element_type=jnp.float32)
        spread = cumul_block.T[:, :, None] - cumul_block.T[:, None, :]
        decay = jnp.where(lower_mask[None], jnp.exp(jnp.where(lower_mask[None], spread, 0.0)), 0.0)
        pair_dot = jnp.einsum(
            "vhp,uhp->hvu", grad_block, input_block, preferred_element_type=jnp.float32
        )
        pair_in = pair_dot * decay * step_block.T[:, None, :]
        pair_all = pair_in * intersection[None]
        head_total = jnp.sum(pair_in, axis=0)
        b_float = b_block.astype(jnp.float32)
        c_float = c_block.astype(jnp.float32)
        input_float = input_block.astype(jnp.float32)
        grad_float = grad_block.astype(jnp.float32)
        growth = jnp.exp(cumul_block)
        shrink = jnp.exp(end_value[None, :] - cumul_block)
        grad_c_rows = jnp.dot(head_total, b_float, precision=highest) + jnp.dot(
            (grad_float * growth[..., None]).reshape(SPAN, -1),
            state_in.reshape(-1, state_dim),
            precision=highest,
        )
        grad_b_rows = jnp.dot(head_total.T, c_float, precision=highest) + jnp.dot(
            (input_float * (step_block * shrink)[..., None]).reshape(SPAN, -1),
            state_out.reshape(-1, state_dim),
            precision=highest,
        )
        mixing = decay * intersection[None]
        adjoint_b = jnp.einsum("hvt,vhp->thp", mixing, grad_float, precision=highest) + shrink[
            ..., None
        ] * jnp.einsum("tn,hpn->thp", b_float, state_out, precision=highest)
        grad_input_rows = step_block[..., None] * adjoint_b + skip_gain[None, :, None] * grad_float
        inner_sum = jnp.cumsum(pair_all, axis=2) - pair_all
        pair_terms = jnp.sum(jnp.where(lower_mask[None], inner_sum, 0.0), axis=1).T
        term_in = growth * jnp.sum(
            jnp.einsum("vhp,hpn->vhn", grad_float, state_in, precision=highest)
            * c_float[:, None, :],
            axis=-1,
        )
        term_out = (
            shrink
            * step_block
            * jnp.sum(
                jnp.einsum("uhp,hpn->uhn", input_float, state_out, precision=highest)
                * b_float[:, None, :],
                axis=-1,
            )
        )
        through = jnp.exp(end_value) * jnp.sum(state_in * state_out, axis=(1, 2))
        later_in = jnp.cumsum(term_in[::-1], axis=0)[::-1]
        earlier_out = jnp.cumsum(term_out, axis=0) - term_out
        decay_grad = pair_terms + later_in + earlier_out + through[None, :]
        step_grad = jnp.sum(input_float * adjoint_b, axis=-1) - decay_rate[None, :] * decay_grad
        raw_grad = step_grad * jax.nn.sigmoid(raw_block)
        return (unused_carry, (grad_input_rows, raw_grad, grad_b_rows, grad_c_rows))

    items = (
        input_blocks,
        grad_blocks,
        b_blocks,
        c_blocks,
        step_blocks,
        raw_blocks,
        cumulative,
        entering,
        leaving,
    )
    unused_final, results = lax.scan(one_block, jnp.zeros((), jnp.float32), items)
    grad_input_all, grad_raw_all, grad_b_all, grad_c_all = results
    grad_inputs = grad_input_all.reshape(tok_rows, head_count * head_width).astype(jnp.bfloat16)
    grad_step_raw = grad_raw_all.reshape(tok_rows, head_count)
    grad_b, grad_c = (
        lax.psum_scatter(
            grad_b_all.reshape(tok_rows, state_dim), "head", scatter_dimension=0, tiled=True
        ),
        lax.psum_scatter(
            grad_c_all.reshape(tok_rows, state_dim), "head", scatter_dimension=0, tiled=True
        ),
    )
    return (grad_inputs, grad_step_raw, grad_b, grad_c)


def solution(mesh):
    placed = (
        P("seq", "head"),
        P("seq", "head"),
        P("seq", None),
        P("seq", None),
        P("seq", "head"),
        P("head"),
        P("head"),
        P("head"),
        P(None, "seq", "head", None),
        P(),
    )
    return jax.shard_map(
        on_device,
        mesh=mesh,
        in_specs=placed,
        out_specs=(
            P("seq", "head"),
            P("seq", "head"),
            P(("seq", "head"), None),
            P(("seq", "head"), None),
        ),
        check_vma=False,
    )
```

profile of v0, /device:TPU:1, one launch (start us, length us, event | category | flops | bytes accessed | tf_op | source)
XLA Modules:
  0.0 402.2 jit_solution(10806171807294314042)
XLA Ops:
  14.7 3.9 copy.103
  18.6 3.3 reshape.231
  24.2 4.6 %fusion.83 = f32[4,16,64,128]{3,2,1,0:T(8,128)} fusion(bf16[4,256,128,1]{2,1,3,0:T(8,128)(2,1)} %bitcast.15, f32[4,256,16,64]{1,0,3,2:T(4,128)S(1)} %convert_multiply_fusion.5), kind=kOutput, calls=%fused_computation.131 | convolution fusion | flops 1610612736 | bytes 6553600 | tf_op jit(solution)/shard_map/cvhp,cvn->chpn/dot_general | solution.py:89
  28.8 7.4 %fusion.85 = f32[16,1,64,128]{3,1,2,0:T(1,128)} fusion(f32[4,16,1,1]{0,2,3,1:T(1,128)S(1)} %copy.128, f32[4,16,64,128]{3,2,1,0:T(8,128)} %fusion.83), kind=kOutput, calls=%fused_computation.135 | convolution fusion | flops 6291456 | bytes 2621696 | tf_op jit(solution)/shard_map/ch,chpn->hpn/dot_general | solution.py:98
  38.5 6.3 %all-to-all-start = ((f32[8,8,16,128]{3,2,1,0:T(8,128)}), f32[8,8,16,128]{3,2,1,0:T(8,128)}, u32[]{:S(2)}, u32[]{:S(2)}) async-start(f32[8,8,16,128]{3,2,1,0:T(8,128)} %broadcast_select_fusion), calls=%async_computation | async-start | bytes 1048576 | tf_op jit(solution)/shard_map/all_to_all | solution.py:61
  44.8 4.0 copy.112
  48.8 4.5 %reshape.237 = bf16[4,256,16,64]{1,0,3,2:T(4,128)(2,1)} reshape(bf16[1024,1024]{0,1:T(8,128)(2,1)} %copy.112) | data formatting | bytes 4194304 | tf_op jit(solution)/shard_map/reshape | solution.py:77
  54.6 4.5 %convert_multiply_fusion.4 = f32[4,256,16,64]{1,0,3,2:T(4,128)} fusion(bf16[4,256,16,64]{1,0,3,2:T(4,128)(2,1)} %reshape.237, f32[4,256,16]{1,0,2:T(4,128)S(1)} %get-tuple-element.568), kind=kLoop, calls=%fused_computation.133 | loop fusion | flops 2097152 | bytes 6356992 | tf_op jit(solution)/shard_map/mul | solution.py:85
  59.1 4.8 %all-to-all-done = f32[8,8,16,128]{3,2,1,0:T(8,128)} async-done(((f32[8,8,16,128]{3,2,1,0:T(8,128)}), f32[8,8,16,128]{3,2,1,0:T(8,128)}, u32[]{:S(2)}, u32[]{:S(2)}) %all-to-all-start) | async-done | bytes 524320 | tf_op jit(solution)/shard_map/all_to_all | solution.py:61
  64.0 12.2 %all-to-all-start.1 = ((f32[1,64,16,128]{3,2,0,1:T(8,128)}), f32[1,64,16,128]{3,2,0,1:T(8,128)S(1)}, u32[]{:S(2)}, u32[]{:S(2)}) async-start(f32[1,64,16,128]{3,2,0,1:T(8,128)} %bitcast.19), calls=%async_computation.1 | async-start | bytes 1048576 | tf_op jit(solution)/shard_map/all_to_all | solution.py:60
  78.9 3.4 copy.120
  82.3 16.2 %all-reduce = f32[128]{0:T(128)S(1)} all-reduce(f32[128]{0:T(128)S(1)} %exponential_dynamic-update-slice_fusion), channel_id=2, replica_groups=mesh['seq'=8,'head'=4] {'seq'}, use_global_device_ids=true, to_apply=%add | all-reduce | flops 128 | bytes 1024
  98.5 6.0 %fusion.81 = f32[4,16,64,128]{3,2,1,0:T(8,128)} fusion(bf16[4,256,128,1]{2,1,3,0:T(8,128)(2,1)} %bitcast.24, f32[4,256,16,64]{1,0,3,2:T(4,128)} %convert_multiply_fusion.4), kind=kOutput, calls=%fused_computation.129 | convolution fusion | flops 1610612736 | bytes 6553600 | tf_op jit(solution)/shard_map/cuhp,cun->chpn/dot_general | solution.py:83
  108.0 8.2 %while.61 = (s32[]{:T(128)}, f32[16,64,128]{2,1,0:T(8,128)S(1)}, f32[4,16,64,128]{3,2,1,0:T(8,128)}, f32[4,16]{1,0:T(4,128)S(1)}, f32[4,16,64,128]{3,2,1,0:T(8,128)}, /*index=5*/s32[]{:T(128)}) while((s32[]{:T(128)}, f32[16,64,128]{2,1,0:T(8,128)S(1)}, f32[4,16,64,128]{3,2,1,0:T(8,128)}, f32[4,16]{1,0:T(4,128)S(1)}, ...), condition=%wide.region_4.5_spmd, body=%wide.region_3.4_spmd.sunk | while | flops 262146 | bytes 2622221 | solution.py:96
  116.2 3.6 all-gather.4.cloned.1.call-done
  119.8 4.7 %rev.13 = f32[8,16,64,128]{3,2,1,0:T(8,128)} reverse(f32[8,16,64,128]{3,2,1,0:T(8,128)} %bitcast.393), dimensions={0} | reverse | bytes 8388608 | tf_op jit(solution)/shard_map/rev | solution.py:15
  124.6 8.5 %while.63 = (s32[]{:T(128)}, f32[16,64,128]{2,1,0:T(8,128)S(1)}, s32[]{:T(128)}, f32[8,16]{1,0:T(8,128)S(1)}, f32[8,16,64,128]{3,2,1,0:T(8,128)}, /*index=5*/s32[]{:T(128)}, s32[]{:T(128)}) while((s32[]{:T(128)}, f32[16,64,128]{2,1,0:T(8,128)S(1)}, s32[]{:T(128)}, f32[8,16]{1,0:T(8,128)S(1)}, f32[8,16,64,128]{3,2,1,0:T(8,128)}, ...), condition=%wide.region_8.9_spmd.clone, body=%wide.region_7.8_spmd.clone.sunk | while | flops 524292 | bytes 1573161 | solution.py:25
  134.7 8.2 %while.60 = (s32[]{:T(128)}, f32[16,64,128]{2,1,0:T(8,128)S(1)}, f32[4,16,64,128]{3,2,1,0:T(8,128)}, f32[4,16]{1,0:T(4,128)S(1)}, f32[4,16,64,128]{3,2,1,0:T(8,128)}, /*index=5*/s32[]{:T(128)}, s32[]{:T(128)}) while((s32[]{:T(128)}, f32[16,64,128]{2,1,0:T(8,128)S(1)}, f32[4,16,64,128]{3,2,1,0:T(8,128)}, f32[4,16]{1,0:T(4,128)S(1)}, ...), condition=%wide.region_10.11_spmd, body=%wide.region_9.10_spmd.sunk | while | flops 262147 | bytes 2621733 | solution.py:102
  142.9 206.6 %while.62 = (s32[]{:T(128)}, bf16[4,256,16,64]{1,3,2,0:T(8,128)(2,1)}, f32[4,256,16]{1,0,2:T(4,128)}, f32[4,256,128]{2,1,0:T(8,128)}, f32[4,256,128]{2,1,0:T(8,1...) while((s32[]{:T(128)}, ...), condition=%wide.region_24.25_spmd.clone.clone, body=%wide.region_11.24_spmd.clone.clone.sunk | while | flops 3331772416 | bytes 88516288 | solution.py:184
  147.3 2.8 fusion.171
  150.1 2.5 fusion.172
  155.6 3.2 fusion.174
  169.1 2.8 fusion.169
  176.2 4.2 %fusion.166 = f32[256,16,64]{0,2,1:T(8,128)S(1)} fusion(f32[256,256]{0,1:T(8,128)} %copy-done.4, f32[16,256]{1,0:T(8,128)} %bitcast.399, pred[256,256]{0,1:T(8,128)(4,1)S(1)} %iota_compare_fusion.2, bf16[4,256,16,64]{1,3,2,0:T(8,128)(2,1)S(1)} %get-tuple-element.908, s32[]{:T(128)} %get-tuple-element.882), kind=kOutput, calls=%fused_computation.35.clone.1 | convolution fusion | flops 809500672 | bytes 1933824 | tf_op jit(solution)/shard_map/while/body/eval_jaxpr/hvt,vhp->thp/dot_general | solution.py:145
  184.8 2.5 fusion.179
  198.9 2.8 fusion.171
  201.7 2.5 fusion.172
  207.2 3.2 fusion.174
  220.7 2.8 fusion.169
  227.8 4.2 %fusion.166 = f32[256,16,64]{0,2,1:T(8,128)S(1)} fusion(f32[256,256]{0,1:T(8,128)} %copy-done.4, f32[16,256]{1,0:T(8,128)} %bitcast.399, pred[256,256]{0,1:T(8,128)(4,1)S(1)} %iota_compare_fusion.2, bf16[4,256,16,64]{1,3,2,0:T(8,128)(2,1)S(1)} %get-tuple-element.908, s32[]{:T(128)} %get-tuple-element.882), kind=kOutput, calls=%fused_computation.35.clone.1 | convolution fusion | flops 809500672 | bytes 1933824 | tf_op jit(solution)/shard_map/while/body/eval_jaxpr/hvt,vhp->thp/dot_general | solution.py:145
  239.2 2.5 fusion.177
  250.5 2.8 fusion.171
  253.3 2.5 fusion.172
  258.9 3.2 fusion.174
  272.3 2.8 fusion.169
  279.5 4.2 %fusion.166 = f32[256,16,64]{0,2,1:T(8,128)S(1)} fusion(f32[256,256]{0,1:T(8,128)} %copy-done.4, f32[16,256]{1,0:T(8,128)} %bitcast.399, pred[256,256]{0,1:T(8,128)(4,1)S(1)} %iota_compare_fusion.2, bf16[4,256,16,64]{1,3,2,0:T(8,128)(2,1)S(1)} %get-tuple-element.908, s32[]{:T(128)} %get-tuple-element.882), kind=kOutput, calls=%fused_computation.35.clone.1 | convolution fusion | flops 809500672 | bytes 1933824 | tf_op jit(solution)/shard_map/while/body/eval_jaxpr/hvt,vhp->thp/dot_general | solution.py:145
  290.8 2.5 fusion.177
  302.2 2.8 fusion.171
  305.0 2.5 fusion.172
  310.5 3.2 fusion.174
  324.0 2.8 fusion.169
  331.1 4.2 %fusion.166 = f32[256,16,64]{0,2,1:T(8,128)S(1)} fusion(f32[256,256]{0,1:T(8,128)} %copy-done.4, f32[16,256]{1,0:T(8,128)} %bitcast.399, pred[256,256]{0,1:T(8,128)(4,1)S(1)} %iota_compare_fusion.2, bf16[4,256,16,64]{1,3,2,0:T(8,128)(2,1)S(1)} %get-tuple-element.908, s32[]{:T(128)} %get-tuple-element.882), kind=kOutput, calls=%fused_computation.35.clone.1 | convolution fusion | flops 809500672 | bytes 1933824 | tf_op jit(solution)/shard_map/while/body/eval_jaxpr/hvt,vhp->thp/dot_general | solution.py:145
  339.7 2.5 fusion.179
  342.5 2.5 fusion.177
  350.2 6.2 %copy.134 = bf16[4,256,16,64]{3,2,1,0:T(8,128)(2,1)} copy(bf16[4,256,16,64]{1,3,2,0:T(8,128)(2,1)} %get-tuple-element.327) | data formatting | bytes 4194304
  356.5 6.6 %reshape.289 = bf16[1024,1024]{1,0:T(8,128)(2,1)} reshape(bf16[4,256,16,64]{3,2,1,0:T(8,128)(2,1)} %copy.134) | data formatting | bytes 4194304
  363.7 7.3 %reduce-scatter.3.cloned.1.call-done = f32[256,128]{1,0:T(8,128)} async-done(((f32[1024,128]{1,0:T(8,128)}), f32[256,128]{1,0:T(8,128)}) %reduce-scatter.3.cloned.1.call-update) | async-done | bytes 131088 | tf_op jit(solution)/shard_map/reduce_scatter | solution.py:189
  370.9 24.8 %reduce-scatter.5.cloned.1.call-done = f32[256,128]{1,0:T(8,128)} async-done(((f32[1024,128]{1,0:T(8,128)}), f32[256,128]{1,0:T(8,128)}) %reduce-scatter.5.cloned.1.call-update) | async-done | bytes 131088 | tf_op jit(solution)/shard_map/reduce_scatter | solution.py:192
  (388 shorter events, 177.6 us)
Async XLA Ops:
  7.2 29.8 %copy-start = (f32[8,8,16,128]{3,2,1,0:T(8,128)S(1)}, f32[8,8,16,128]{3,2,1,0:T(8,128)}, u32[]{:S(2)}) copy-start(f32[8,8,16,128]{3,2,1,0:T(8,128)} %param.26) | copy-start | bytes 1572868
  7.2 112.7 %all-gather.4.cloned.1.call-start = ((), (), s32[]{:S(2)}) async-start(), calls=%async_computation.6 | async-start | bytes 4718592 | tf_op jit(solution)/shard_map/all_gather | solution.py:14
  22.0 31.4 %copy-start.2 = (bf16[4,256,16,64]{1,0,3,2:T(4,128)(2,1)}, bf16[4,256,16,64]{1,0,3,2:T(4,128)(2,1)S(1)}, u32[]{:S(2)}) copy-start(bf16[4,256,16,64]{1,0,3,2:T(4,128)(2,1)S(1)} %reshape.231) | copy-start | bytes 6291460
  24.2 12.1 %copy-start.19 = (s32[8]{0:T(128)S(1)}, s32[8]{0:T(128)}, u32[]{:S(2)}) copy-start(s32[8]{0:T(128)} %param.27) | copy-start | bytes 100
  38.5 25.5 %all-to-all-start = ((f32[8,8,16,128]{3,2,1,0:T(8,128)}), f32[8,8,16,128]{3,2,1,0:T(8,128)}, u32[]{:S(2)}, u32[]{:S(2)}) async-start(f32[8,8,16,128]{3,2,1,0:T(8,128)} %broadcast_select_fusion), calls=%async_computation | async-start | bytes 1048576 | tf_op jit(solution)/shard_map/all_to_all | solution.py:61
  44.8 8.5 %copy-start.20 = (u32[32]{0:T(128)S(1)}, u32[32]{0:T(128)}, u32[]{:S(2)}) copy-start(u32[32]{0:T(128)} %constant.147) | copy-start | bytes 388
  64.0 40.6 %all-to-all-start.1 = ((f32[1,64,16,128]{3,2,0,1:T(8,128)}), f32[1,64,16,128]{3,2,0,1:T(8,128)S(1)}, u32[]{:S(2)}, u32[]{:S(2)}) async-start(f32[1,64,16,128]{3,2,0,1:T(8,128)} %bitcast.19), calls=%async_computation.1 | async-start | bytes 1048576 | tf_op jit(solution)/shard_map/all_to_all | solution.py:60
  76.2 294.8 %reduce-scatter.3.cloned.1.call-start = ((), (), s32[]{:S(2)}) async-start(), calls=%async_computation.4 | async-start | bytes 655360 | tf_op jit(solution)/shard_map/reduce_scatter | solution.py:189
  145.8 9.8 %copy-start.5 = (f32[1,256,16]{1,2,0:T(8,128)}, f32[1,256,16]{1,2,0:T(8,128)S(1)}, u32[]{:S(2)}) copy-start(f32[1,256,16]{1,2,0:T(8,128)S(1)} %copy.216) | copy-start | bytes 49156 | tf_op jit(solution)/shard_map/while
  174.6 5.8 %copy-start.9 = (bf16[4,256,16,64]{1,3,2,0:T(8,128)(2,1)S(1)}, bf16[4,256,16,64]{1,3,2,0:T(8,128)(2,1)}, u32[]{:S(2)}) copy-start(bf16[4,256,16,64]{1,3,2,0:T(8,128)(2,1)} %get-tuple-element.883) | copy-start | bytes 6291460 | tf_op jit(solution)/shard_map/while
  174.6 5.8 %copy-start.16 = (f32[16]{0:T(128)S(1)}, f32[16]{0:T(128)}, u32[]{:S(2)}) copy-start(f32[16]{0:T(128)} %get-tuple-element.913) | copy-start | bytes 196 | tf_op jit(solution)/shard_map/while
  183.3 6.8 %copy-start.13 = (f32[256,16]{0,1:T(8,128)S(1)}, f32[256,16]{0,1:T(8,128)}, u32[]{:S(2)}) copy-start(f32[256,16]{0,1:T(8,128)} %get-tuple-element.789) | copy-start | bytes 49156 | tf_op jit(solution)/shard_map/while
  183.3 7.9 %copy-start.6 = (f32[256,16]{0,1:T(8,128)S(1)}, f32[256,16]{0,1:T(8,128)}, u32[]{:S(2)}) copy-start(f32[256,16]{0,1:T(8,128)} %get-tuple-element.788) | copy-start | bytes 49156 | tf_op jit(solution)/shard_map/while
  183.3 8.7 %copy-start.15 = (f32[1,1,16]{2,1,0:T(1,128)S(1)}, f32[1,1,16]{2,1,0:T(1,128)}, u32[]{:S(2)}) copy-start(f32[1,1,16]{2,1,0:T(1,128)} %copy.219) | copy-start | bytes 196 | tf_op jit(solution)/shard_map/while
  183.3 8.7 %copy-start.18 = (f32[16]{0:T(128)S(1)}, f32[16]{0:T(128)}, u32[]{:S(2)}) copy-start(f32[16]{0:T(128)} %get-tuple-element.793) | copy-start | bytes 196 | tf_op jit(solution)/shard_map/while
  183.3 9.6 %copy-start.12 = (f32[16,256]{1,0:T(8,128)S(1)}, f32[16,256]{1,0:T(8,128)}, u32[]{:S(2)}) copy-start(f32[16,256]{1,0:T(8,128)} %get-tuple-element.792) | copy-start | bytes 49156 | tf_op jit(solution)/shard_map/while
  183.3 9.6 %copy-start.17 = (f32[16]{0:T(128)S(1)}, f32[16]{0:T(128)}, u32[]{:S(2)}) copy-start(f32[16]{0:T(128)} %get-tuple-element.915) | copy-start | bytes 196 | tf_op jit(solution)/shard_map/while
  196.4 5.2 %copy-start.4 = (f32[256,256]{0,1:T(8,128)}, f32[256,256]{0,1:T(8,128)S(1)}, u32[]{:S(2)}) copy-start(f32[256,256]{0,1:T(8,128)S(1)} %fusion.165) | copy-start | bytes 786436 | tf_op jit(solution)/shard_map/while
  197.4 9.8 %copy-start.5 = (f32[1,256,16]{1,2,0:T(8,128)}, f32[1,256,16]{1,2,0:T(8,128)S(1)}, u32[]{:S(2)}) copy-start(f32[1,256,16]{1,2,0:T(8,128)S(1)} %copy.216) | copy-start | bytes 49156 | tf_op jit(solution)/shard_map/while
  226.2 5.8 %copy-start.9 = (bf16[4,256,16,64]{1,3,2,0:T(8,128)(2,1)S(1)}, bf16[4,256,16,64]{1,3,2,0:T(8,128)(2,1)}, u32[]{:S(2)}) copy-start(bf16[4,256,16,64]{1,3,2,0:T(8,128)(2,1)} %get-tuple-element.883) | copy-start | bytes 6291460 | tf_op jit(solution)/shard_map/while
  226.2 5.8 %copy-start.16 = (f32[16]{0:T(128)S(1)}, f32[16]{0:T(128)}, u32[]{:S(2)}) copy-start(f32[16]{0:T(128)} %get-tuple-element.913) | copy-start | bytes 196 | tf_op jit(solution)/shard_map/while
  234.9 6.8 %copy-start.13 = (f32[256,16]{0,1:T(8,128)S(1)}, f32[256,16]{0,1:T(8,128)}, u32[]{:S(2)}) copy-start(f32[256,16]{0,1:T(8,128)} %get-tuple-element.789) | copy-start | bytes 49156 | tf_op jit(solution)/shard_map/while
  234.9 7.9 %copy-start.6 = (f32[256,16]{0,1:T(8,128)S(1)}, f32[256,16]{0,1:T(8,128)}, u32[]{:S(2)}) copy-start(f32[256,16]{0,1:T(8,128)} %get-tuple-element.788) | copy-start | bytes 49156 | tf_op jit(solution)/shard_map/while
  234.9 8.7 %copy-start.15 = (f32[1,1,16]{2,1,0:T(1,128)S(1)}, f32[1,1,16]{2,1,0:T(1,128)}, u32[]{:S(2)}) copy-start(f32[1,1,16]{2,1,0:T(1,128)} %copy.219) | copy-start | bytes 196 | tf_op jit(solution)/shard_map/while
  234.9 8.7 %copy-start.18 = (f32[16]{0:T(128)S(1)}, f32[16]{0:T(128)}, u32[]{:S(2)}) copy-start(f32[16]{0:T(128)} %get-tuple-element.793) | copy-start | bytes 196 | tf_op jit(solution)/shard_map/while
  234.9 9.6 %copy-start.12 = (f32[16,256]{1,0:T(8,128)S(1)}, f32[16,256]{1,0:T(8,128)}, u32[]{:S(2)}) copy-start(f32[16,256]{1,0:T(8,128)} %get-tuple-element.792) | copy-start | bytes 49156 | tf_op jit(solution)/shard_map/while
  234.9 9.6 %copy-start.17 = (f32[16]{0:T(128)S(1)}, f32[16]{0:T(128)}, u32[]{:S(2)}) copy-start(f32[16]{0:T(128)} %get-tuple-element.915) | copy-start | bytes 196 | tf_op jit(solution)/shard_map/while
  249.0 9.8 %copy-start.5 = (f32[1,256,16]{1,2,0:T(8,128)}, f32[1,256,16]{1,2,0:T(8,128)S(1)}, u32[]{:S(2)}) copy-start(f32[1,256,16]{1,2,0:T(8,128)S(1)} %copy.216) | copy-start | bytes 49156 | tf_op jit(solution)/shard_map/while
  277.9 5.8 %copy-start.9 = (bf16[4,256,16,64]{1,3,2,0:T(8,128)(2,1)S(1)}, bf16[4,256,16,64]{1,3,2,0:T(8,128)(2,1)}, u32[]{:S(2)}) copy-start(bf16[4,256,16,64]{1,3,2,0:T(8,128)(2,1)} %get-tuple-element.883) | copy-start | bytes 6291460 | tf_op jit(solution)/shard_map/while
  277.9 5.8 %copy-start.16 = (f32[16]{0:T(128)S(1)}, f32[16]{0:T(128)}, u32[]{:S(2)}) copy-start(f32[16]{0:T(128)} %get-tuple-element.913) | copy-start | bytes 196 | tf_op jit(solution)/shard_map/while
  286.5 6.8 %copy-start.13 = (f32[256,16]{0,1:T(8,128)S(1)}, f32[256,16]{0,1:T(8,128)}, u32[]{:S(2)}) copy-start(f32[256,16]{0,1:T(8,128)} %get-tuple-element.789) | copy-start | bytes 49156 | tf_op jit(solution)/shard_map/while
  286.5 7.9 %copy-start.6 = (f32[256,16]{0,1:T(8,128)S(1)}, f32[256,16]{0,1:T(8,128)}, u32[]{:S(2)}) copy-start(f32[256,16]{0,1:T(8,128)} %get-tuple-element.788) | copy-start | bytes 49156 | tf_op jit(solution)/shard_map/while
  286.5 8.7 %copy-start.15 = (f32[1,1,16]{2,1,0:T(1,128)S(1)}, f32[1,1,16]{2,1,0:T(1,128)}, u32[]{:S(2)}) copy-start(f32[1,1,16]{2,1,0:T(1,128)} %copy.219) | copy-start | bytes 196 | tf_op jit(solution)/shard_map/while
  286.6 8.7 %copy-start.18 = (f32[16]{0:T(128)S(1)}, f32[16]{0:T(128)}, u32[]{:S(2)}) copy-start(f32[16]{0:T(128)} %get-tuple-element.793) | copy-start | bytes 196 | tf_op jit(solution)/shard_map/while
  286.6 9.6 %copy-start.12 = (f32[16,256]{1,0:T(8,128)S(1)}, f32[16,256]{1,0:T(8,128)}, u32[]{:S(2)}) copy-start(f32[16,256]{1,0:T(8,128)} %get-tuple-element.792) | copy-start | bytes 49156 | tf_op jit(solution)/shard_map/while
  286.6 9.6 %copy-start.17 = (f32[16]{0:T(128)S(1)}, f32[16]{0:T(128)}, u32[]{:S(2)}) copy-start(f32[16]{0:T(128)} %get-tuple-element.915) | copy-start | bytes 196 | tf_op jit(solution)/shard_map/while
  300.7 9.8 %copy-start.5 = (f32[1,256,16]{1,2,0:T(8,128)}, f32[1,256,16]{1,2,0:T(8,128)S(1)}, u32[]{:S(2)}) copy-start(f32[1,256,16]{1,2,0:T(8,128)S(1)} %copy.216) | copy-start | bytes 49156 | tf_op jit(solution)/shard_map/while
  329.5 5.8 %copy-start.9 = (bf16[4,256,16,64]{1,3,2,0:T(8,128)(2,1)S(1)}, bf16[4,256,16,64]{1,3,2,0:T(8,128)(2,1)}, u32[]{:S(2)}) copy-start(bf16[4,256,16,64]{1,3,2,0:T(8,128)(2,1)} %get-tuple-element.883) | copy-start | bytes 6291460 | tf_op jit(solution)/shard_map/while
  329.5 5.8 %copy-start.16 = (f32[16]{0:T(128)S(1)}, f32[16]{0:T(128)}, u32[]{:S(2)}) copy-start(f32[16]{0:T(128)} %get-tuple-element.913) | copy-start | bytes 196 | tf_op jit(solution)/shard_map/while
  338.2 6.8 %copy-start.13 = (f32[256,16]{0,1:T(8,128)S(1)}, f32[256,16]{0,1:T(8,128)}, u32[]{:S(2)}) copy-start(f32[256,16]{0,1:T(8,128)} %get-tuple-element.789) | copy-start | bytes 49156 | tf_op jit(solution)/shard_map/while
  338.2 7.9 %copy-start.6 = (f32[256,16]{0,1:T(8,128)S(1)}, f32[256,16]{0,1:T(8,128)}, u32[]{:S(2)}) copy-start(f32[256,16]{0,1:T(8,128)} %get-tuple-element.788) | copy-start | bytes 49156 | tf_op jit(solution)/shard_map/while
  338.2 8.7 %copy-start.15 = (f32[1,1,16]{2,1,0:T(1,128)S(1)}, f32[1,1,16]{2,1,0:T(1,128)}, u32[]{:S(2)}) copy-start(f32[1,1,16]{2,1,0:T(1,128)} %copy.219) | copy-start | bytes 196 | tf_op jit(solution)/shard_map/while
  338.2 8.7 %copy-start.18 = (f32[16]{0:T(128)S(1)}, f32[16]{0:T(128)}, u32[]{:S(2)}) copy-start(f32[16]{0:T(128)} %get-tuple-element.793) | copy-start | bytes 196 | tf_op jit(solution)/shard_map/while
  338.2 9.6 %copy-start.12 = (f32[16,256]{1,0:T(8,128)S(1)}, f32[16,256]{1,0:T(8,128)}, u32[]{:S(2)}) copy-start(f32[16,256]{1,0:T(8,128)} %get-tuple-element.792) | copy-start | bytes 49156 | tf_op jit(solution)/shard_map/while
  338.2 9.6 %copy-start.17 = (f32[16]{0:T(128)S(1)}, f32[16]{0:T(128)}, u32[]{:S(2)}) copy-start(f32[16]{0:T(128)} %get-tuple-element.915) | copy-start | bytes 196 | tf_op jit(solution)/shard_map/while
  349.5 46.2 %reduce-scatter.5.cloned.1.call-start = ((), (), s32[]{:S(2)}) async-start(), calls=%async_computation.5 | async-start | bytes 655360 | tf_op jit(solution)/shard_map/reduce_scatter | solution.py:192
  350.2 45.5 %copy-start.1 = (f32[8,8,16,128]{3,2,1,0:T(8,128)S(1)}, f32[8,8,16,128]{3,2,1,0:T(8,128)}, u32[]{:S(2)}) copy-start(f32[8,8,16,128]{3,2,1,0:T(8,128)} %param.26) | copy-start | bytes 1572868
  356.5 6.6 %copy-start.14 = (f32[4,256,16]{1,0,2:T(4,128)S(1)}, f32[4,256,16]{1,0,2:T(4,128)}, u32[]{:S(2)}) copy-start(f32[4,256,16]{1,0,2:T(4,128)} %get-tuple-element.328) | copy-start | bytes 196612
  (20 other events, 59.0 us)
Sparse Core Ops, SparseCore 0:
  36.4 83.4 all-gather.3
  349.6 21.2 reduce-scatter.2
  374.0 21.6 reduce-scatter.4
where the time goes:
time: 408 us; the launch traced here: 402 us
  local copies, waits for them, and re-layouts  117 us (29%)
  matrix products  103 us (25%)
  other arithmetic  90.9 us (22%)
  waiting for transfers between devices  41.2 us (10%)
  starting transfers between devices  18.6 us (5%)
  blocking collectives  16.2 us (4%)
  between operations  14.6 us (4%)
    unnamed x24, local copies, waits for them, and re-layouts  28.2 us
    reduce_scatter x1, waiting for transfers between devices, on_device(): lax.psum_scatter(grad_c_all.reshape(tok_rows, state_dim), 'head', scatter...  24.8 us
    another operation x37, other arithmetic  19.9 us
    dynamic_slice x28, local copies, waits for them, and re-layouts, on_device(): lax.scan(one_block, jnp.zeros((), jnp.float32), items)  17 us
    dot_general x4, matrix products, one_block(): jnp.einsum('hvt,vhp->thp', mixing, grad_float, precision=highest)  16.7 us
    unnamed x1, blocking collectives  16.2 us
    another operation x41, local copies, waits for them, and re-layouts  15.2 us
    while x116, local copies, waits for them, and re-layouts  13 us
  transfers between devices with their start and end apart: 5, of which 4 were waited for; matrix products, arithmetic and copies ran while one was open for 13% of the time, Pallas kernels for 0%

commit v1 on v0

v1 whole, which is shorter than its diff:
```python
import functools
import math

import jax
import jax.numpy as jnp
from jax import lax
from jax.experimental import pallas as pl
from jax.experimental.pallas import tpu as pltpu
from jax.sharding import PartitionSpec as P

MESH = pl.DeviceIdType.MESH
LB = 128
f32, bf16 = jnp.float32, jnp.bfloat16
LOG2E = math.log2(math.e)


def mm(a, b):
    return jnp.dot(a, b, preferred_element_type=f32)


def mm_nt(a, b):
    return lax.dot_general(a, b, (((1,), (1,)), ((), ())), preferred_element_type=f32)


def split(v):
    hi = v.astype(bf16)
    return hi, (v - hi.astype(f32)).astype(bf16)


def mm2(v, b):
    hi, lo = split(v)
    return mm(hi, b) + mm(lo, b)


def mm_exact(tri, v):
    hi = v.astype(bf16)
    rest = v - hi.astype(f32)
    mid = rest.astype(bf16)
    low = (rest - mid.astype(f32)).astype(bf16)
    return mm(tri, hi) + mm(tri, mid) + mm(tri, low)


def kernel(
    S,
    HD,
    x_ref,
    dy_ref,
    b_ref,
    c_ref,
    raw_ref,
    rate_ref,
    bias_ref,
    skip_ref,
    start,
    gin_ref,
    graw_ref,
    gb_ref,
    gc_ref,
    dys,
    xs,
    dsx,
    decx,
    gpart,
    fpart,
    states,
    adj,
    ecol,
    crow,
    dtc,
    yrow,
    yint,
    gbacc,
    gcacc,
    dsum,
    xrecv,
    zsend,
    zrecv,
    bsend,
    rown,
    rback,
    gbrecv,
    gcrecv,
    expm,
    redm,
    x_send,
    x_recv,
    z_send,
    z_recv,
    b_send,
    b_recv,
    gb_send,
    gb_recv,
    gc_send,
    gc_recv,
):
    T, HP = x_ref.shape
    heads = raw_ref.shape[1]
    width = HP // heads
    nstate = b_ref.shape[1]
    nblk = T // LB
    pairs = HP // 128
    per = 128 // width
    half = pairs // 2
    s = lax.axis_index("seq")
    hd = lax.axis_index("head")
    xx = lax.rem(s, 2)
    zz = s // 2
    Z = S // 2
    rows_out = T // HD

    barrier = pltpu.get_barrier_semaphore()

    def greet(i, _):
        a, b = i // HD, lax.rem(i, HD)

        @pl.when(jnp.logical_or(a != s, b != hd))
        def _():
            pl.semaphore_signal(barrier, inc=1, device_id=(a, b), device_id_type=MESH)

        return 0

    lax.fori_loop(0, S * HD, greet, 0)

    @pl.when(zz == Z - 1)
    def _():
        zrecv[...] = jnp.zeros(zrecv.shape, f32)

    lane_head = lax.broadcasted_iota(jnp.int32, (heads, HP), 1) // width
    expm[...] = (lane_head == lax.broadcasted_iota(jnp.int32, (heads, HP), 0)).astype(f32).astype(bf16)
    row_head = lax.broadcasted_iota(jnp.int32, (HP, heads), 0) // width
    redm[...] = (row_head == lax.broadcasted_iota(jnp.int32, (HP, heads), 1)).astype(f32).astype(bf16)

    iu = lax.broadcasted_iota(jnp.int32, (LB, LB), 0)
    iv = lax.broadcasted_iota(jnp.int32, (LB, LB), 1)
    tril = (iu >= iv).astype(f32).astype(bf16)
    triu = (iu <= iv).astype(f32).astype(bf16)

    rate = jnp.exp(rate_ref[...])
    bias = bias_ref[...]

    def prep(c, _):
        rows = pl.ds(pl.multiple_of(c * LB, LB), LB)
        raw = raw_ref[rows, :] + bias
        z = jnp.exp(-jnp.abs(raw))
        small = z * (1.0 - z * (0.5 - z * (1.0 / 3.0 - 0.25 * z)))
        dt = jnp.maximum(raw, 0.0) + jnp.where(z < 0.02, small, jnp.log(1.0 + z))
        cum = mm_exact(tril, dt * (-LOG2E * rate))
        end = cum[LB - 1 : LB, :]
        growth = jnp.exp2(cum)
        ds = dt * jnp.exp2(end - cum)
        dtc[rows, :] = dt
        ecol[rows, :] = cum - LOG2E * jnp.log(dt)
        crow[c] = cum.T
        gx = mm2(growth, expm[...])
        decx[c] = gx[LB - 1 : LB, :]
        dx = mm2(ds, expm[...])
        dsx[rows, :] = dx
        hi, lo = split(dy_ref[rows, :].astype(f32) * gx)
        dys[c, pl.ds(0, LB), :] = hi
        dys[c, pl.ds(LB, LB), :] = lo
        ct = c_ref[rows, :].astype(f32).T.astype(bf16)
        gpart[c] = mm(jnp.concatenate([ct, ct], axis=1), dys[c])
        return 0

    lax.fori_loop(0, nblk, prep, 0)

    for j in range(pairs):
        cols = pl.ds(128 * j, 128)

        def to_left(i, carry, cols=cols):
            c = nblk - 1 - i
            total, decay = carry
            d = decx[c, :, cols]
            return gpart[c, :, cols] + d * total, decay * d

        total, decay = lax.fori_loop(
            0, nblk, to_left, (jnp.zeros((nstate, 128), f32), jnp.ones((1, 128), f32))
        )
        dsum[j, pl.ds(0, nstate), :] = total
        dsum[j, pl.ds(nstate, 8), :] = jnp.broadcast_to(decay, (8, 128))

    pl.semaphore_wait(barrier, S * HD - 1)

    def x_copy(k):
        return pltpu.make_async_remote_copy(
            src_ref=dsum.at[(1 - xx) * half + k],
            dst_ref=xrecv.at[k],
            send_sem=x_send.at[k],
            recv_sem=x_recv.at[k],
            device_id=(s + 1 - 2 * xx, hd),
            device_id_type=MESH,
        )

    for k in range(half):
        x_copy(k).start()

    def z_copy(k):
        return pltpu.make_async_remote_copy(
            src_ref=zsend.at[k],
            dst_ref=zrecv.at[k],
            send_sem=z_send.at[k],
            recv_sem=z_recv.at[k],
            device_id=(s - 2, hd),
            device_id_type=MESH,
        )

    def b_copy(k):
        return pltpu.make_async_remote_copy(
            src_ref=bsend.at[k],
            dst_ref=rback.at[k],
            send_sem=b_send.at[k],
            recv_sem=b_recv.at[k],
            device_id=(s + 1 - 2 * xx, hd),
            device_id_type=MESH,
        )

    def link(k):
        x_copy(k).wait_recv()

        @pl.when(zz < Z - 1)
        def _():
            z_copy(k).wait_recv()

        own = xx * half + k
        first = xx == 0
        m_sum = dsum[own, pl.ds(0, nstate), :]
        m_dec = dsum[own, pl.ds(nstate, 1), :]
        t_sum = xrecv[k, pl.ds(0, nstate), :]
        t_dec = xrecv[k, pl.ds(nstate, 1), :]
        incoming = zrecv[k]
        later = jnp.where(first, t_sum, m_sum)
        later_dec = jnp.where(first, t_dec, m_dec)
        early = jnp.where(first, m_sum, t_sum)
        early_dec = jnp.where(first, m_dec, t_dec)
        middle = later + later_dec * incoming
        zsend[k] = early + early_dec * middle

        @pl.when(zz > 0)
        def _():
            z_copy(k).start()

        rown[k] = jnp.where(first, middle, incoming)
        bsend[k] = jnp.where(first, incoming, middle)
        b_copy(k).start()

    masks = [
        (lax.broadcasted_iota(jnp.int32, (1, 128), 1) // width == a).astype(f32).astype(bf16)
        for a in range(per)
    ]
    reach = iv >= iu

    def intra(c, _):
        rows = pl.ds(pl.multiple_of(c * LB, LB), LB)
        b = b_ref[rows, :]
        cc = c_ref[rows, :]
        cbt = mm_nt(b, cc)
        ec = ecol[rows, :]
        head_total = jnp.zeros((LB, LB), f32)
        for j in range(pairs):
            cols = slice(128 * j, 128 * j + 128)
            xp = x_ref[rows, cols]
            dyp = dy_ref[rows, cols]
            dyst = jnp.concatenate([dyp * m for m in masks], axis=0)
            dots = mm_nt(xp, dyst)
            his, los = [], []
            for a in range(per):
                h = per * j + a
                spread = crow[c, pl.ds(h, 1), :] - ec[:, h : h + 1]
                decay = jnp.exp2(jnp.where(reach, spread, -1e30))
                hi, lo = split(decay * cbt)
                his.append(hi)
                los.append(lo)
                pair_in = dots[:, LB * a : LB * a + LB] * decay
                head_total = head_total + pair_in
                yrow[c, pl.ds(h, 1), :] = jnp.sum(pair_in * cbt, axis=0, keepdims=True)
            both = jnp.concatenate(
                [jnp.concatenate(his, axis=1), jnp.concatenate(los, axis=1)], axis=0
            )
            res = mm(both, dyst)
            adj[rows, cols] = res[:LB] + res[LB:]
        gbacc[rows, :] = mm2(head_total, cc)
        gcacc[rows, :] = mm2(head_total.T, b)
        dx = dsx[rows, :]
        hi, lo = split(x_ref[rows, :].astype(f32) * dx)
        xs[c, pl.ds(0, LB), :] = hi
        xs[c, pl.ds(LB, LB), :] = lo
        bt = b.astype(f32).T.astype(bf16)
        fpart[c] = mm(jnp.concatenate([bt, bt], axis=1), xs[c])
        return 0

    lax.fori_loop(0, nblk, intra, 0)

    for j in range(pairs):
        block = start[per * j : per * j + per].reshape(128, nstate)
        states[0, :, 128 * j : 128 * j + 128] = block.T

    def forward(c, _):
        rows = pl.ds(pl.multiple_of(c * LB, LB), LB)
        cc = c_ref[rows, :]
        state = states[c]
        states[c + 1] = decx[c] * state + fpart[c]
        hi, lo = split(state)
        st2 = jnp.concatenate([hi, lo], axis=0)
        sc = mm(jnp.concatenate([cc, cc], axis=1), st2)
        d_hi = dys[c, pl.ds(0, LB), :]
        d_lo = dys[c, pl.ds(LB, LB), :]
        r1 = mm_nt(d_hi, st2)
        gcacc[rows, :] = (
            gcacc[rows, :] + r1[:, :nstate] + r1[:, nstate:] + mm_nt(d_lo, hi)
        )
        prod = (d_hi.astype(f32) + d_lo.astype(f32)) * sc
        yint[rows, :] = mm2(prod, redm[...])
        return 0

    lax.fori_loop(0, nblk, forward, 0)

    def send_out(acc, recv, ssem, rsem, d):
        to = lax.rem(hd + d, HD)
        return pltpu.make_async_remote_copy(
            src_ref=acc.at[pl.ds(pl.multiple_of(to * rows_out, 8), rows_out), :],
            dst_ref=recv.at[d - 1],
            send_sem=ssem.at[d - 1],
            recv_sem=rsem.at[d - 1],
            device_id=(s, to),
            device_id_type=MESH,
        )

    for d in range(1, HD):
        send_out(gcacc, gcrecv, gc_send, gc_recv, d).start()

    for k in range(half):
        link(k)

    hi = skip_ref[...].astype(bf16)
    rem1 = skip_ref[...] - hi.astype(f32)
    mid = rem1.astype(bf16)
    skipx = mm(hi, expm[...]) + mm(mid, expm[...])

    own_half = jnp.concatenate([rown[k] for k in range(half)], axis=1)
    for k in range(half):
        b_copy(k).wait_recv()
    other_half = jnp.concatenate([rback[k] for k in range(half)], axis=1)
    adjoint = jnp.concatenate(
        [jnp.where(xx == 0, own_half, other_half), jnp.where(xx == 0, other_half, own_half)],
        axis=1,
    )

    per_out = nblk // HD

    states_g = fpart
    states_g[0] = adjoint

    def back_block(c):
        rows = pl.ds(pl.multiple_of(c * LB, LB), LB)
        b = b_ref[rows, :]
        g = states_g[0]
        through = jnp.sum(g * states[c + 1], axis=0, keepdims=True)
        hi, lo = split(g)
        g2 = jnp.concatenate([hi, lo], axis=0)
        bg = mm(jnp.concatenate([b, b], axis=1), g2)
        ab = adj[rows, :] + dsx[rows, :] * bg
        dyf = dy_ref[rows, :].astype(f32)
        gin_ref[rows, :] = (ab + skipx * dyf).astype(bf16)
        zz_sum = mm2(x_ref[rows, :].astype(f32) * ab, redm[...])
        x_hi = xs[c, pl.ds(0, LB), :]
        x_lo = xs[c, pl.ds(LB, LB), :]
        r1 = mm_nt(x_hi, g2)
        gbacc[rows, :] = gbacc[rows, :] + r1[:, :nstate] + r1[:, nstate:] + mm_nt(x_lo, hi)
        w_end = mm2(jnp.broadcast_to(through, (8, HP)), redm[...])[0:1, :]
        y_sum = yrow[c].T + yint[rows, :]
        w = w_end + mm_exact(triu, y_sum - zz_sum)
        raw = raw_ref[rows, :] + bias
        graw_ref[rows, :] = (zz_sum / dtc[rows, :] - rate * w) / (1.0 + jnp.exp(-raw))
        states_g[0] = gpart[c] + decx[c] * g

    def back(i, _):
        j = HD - 1 - i

        def inner(q, _):
            back_block(j * per_out + per_out - 1 - q)
            return 0

        lax.fori_loop(0, per_out, inner, 0)

        return 0

    lax.fori_loop(0, HD, back, 0)
    for d in range(1, HD):
        send_out(gbacc, gbrecv, gb_send, gb_recv, d).start()

    own_rows = pl.ds(pl.multiple_of(hd * rows_out, 8), rows_out)
    for acc, recv, ssem, rsem, out in (
        (gcacc, gcrecv, gc_send, gc_recv, gc_ref),
        (gbacc, gbrecv, gb_send, gb_recv, gb_ref),
    ):
        total = acc[own_rows, :]
        for d in range(1, HD):
            send_out(acc, recv, ssem, rsem, d).wait_recv()
            total = total + recv[d - 1]
        out[...] = total

    for d in range(1, HD):
        send_out(gcacc, gcrecv, gc_send, gc_recv, d).wait_send()
        send_out(gbacc, gbrecv, gb_send, gb_recv, d).wait_send()

    for k in range(half):
        x_copy(k).wait_send()
        b_copy(k).wait_send()

        @pl.when(zz > 0)
        def _(k=k):
            z_copy(k).wait_send()


def on_device(S, HD, inputs, out_grad, b, c, raw, log_rate, bias, skip, saved, slot):
    T, HP = inputs.shape
    heads = raw.shape[1]
    width = HP // heads
    N = b.shape[1]
    nblk = T // LB
    pairs = HP // 128
    half = pairs // 2
    inverse = jnp.zeros((S,), jnp.int32).at[slot].set(jnp.arange(S, dtype=jnp.int32))
    ordered = jnp.take(saved, inverse, axis=0)
    start = lax.all_to_all(
        lax.all_to_all(ordered, "seq", split_axis=0, concat_axis=1, tiled=True),
        "head",
        split_axis=1,
        concat_axis=2,
        tiled=True,
    )[0]
    vm = pl.BlockSpec(memory_space=pltpu.VMEM)
    dma = lambda n: pltpu.SemaphoreType.DMA((n,))
    V = pltpu.VMEM
    return pl.pallas_call(
        functools.partial(kernel, S, HD),
        out_shape=(
            jax.ShapeDtypeStruct((T, HP), bf16),
            jax.ShapeDtypeStruct((T, heads), f32),
            jax.ShapeDtypeStruct((T // HD, N), f32),
            jax.ShapeDtypeStruct((T // HD, N), f32),
        ),
        in_specs=[vm] * 9,
        out_specs=(vm, vm, vm, vm),
        scratch_shapes=[
            V((nblk, 2 * LB, HP), bf16),
            V((nblk, 2 * LB, HP), bf16),
            V((T, HP), f32),
            V((nblk, 1, HP), f32),
            V((nblk, N, HP), f32),
            V((nblk, N, HP), f32),
            V((nblk + 1, N, HP), f32),
            V((T, HP), f32),
            V((T, heads), f32),
            V((nblk, heads, LB), f32),
            V((T, heads), f32),
            V((nblk, heads, LB), f32),
            V((T, heads), f32),
            V((T, N), f32),
            V((T, N), f32),
            V((pairs, N + 8, 128), f32),
            V((half, N + 8, 128), f32),
            V((half, N, 128), f32),
            V((half, N, 128), f32),
            V((half, N, 128), f32),
            V((half, N, 128), f32),
            V((half, N, 128), f32),
            V((HD - 1, T // HD, N), f32),
            V((HD - 1, T // HD, N), f32),
            V((heads, HP), bf16),
            V((HP, heads), bf16),
            dma(half),
            dma(half),
            dma(half),
            dma(half),
            dma(half),
            dma(half),
            dma(HD - 1),
            dma(HD - 1),
            dma(HD - 1),
            dma(HD - 1),
        ],
        compiler_params=pltpu.CompilerParams(
            collective_id=0, has_side_effects=True, vmem_limit_bytes=60 * 1024 * 1024
        ),
        name="ssm_backward",
    )(
        inputs,
        out_grad,
        b,
        c,
        raw,
        log_rate.reshape(1, heads),
        bias.reshape(1, heads),
        skip.reshape(1, heads),
        start,
    )


def solution(mesh):
    placed = (
        P("seq", "head"),
        P("seq", "head"),
        P("seq", None),
        P("seq", None),
        P("seq", "head"),
        P("head"),
        P("head"),
        P("head"),
        P(None, "seq", "head", None),
        P(),
    )
    return jax.shard_map(
        functools.partial(on_device, mesh.shape["seq"], mesh.shape["head"]),
        mesh=mesh,
        in_specs=placed,
        out_specs=(
            P("seq", "head"),
            P("seq", "head"),
            P(("seq", "head"), None),
            P(("seq", "head"), None),
        ),
        check_vma=False,
    )
```

time: 408 us -> 98.2 us (0.24); the launches traced: 402 us -> 97.9 us
  local copies, waits for them, and re-layouts: 117 us -> 9.32 us
  matrix products: 103 us -> 0 us
  other arithmetic: 90.9 us -> 0.84 us
  Pallas kernels: 0 us -> 55 us
  waiting for transfers between devices: 41.2 us -> 6.85 us
  between operations: 14.6 us -> 0.71 us
  starting transfers between devices: 18.6 us -> 5.23 us
    dot_general x43 -> x0, matrix products: 103 us -> none  [the longest x4 16.7 us: one_block(): jnp.einsum('hvt,vhp->thp', mixing, grad_float, precision=highest)]
    pallas_call x0 -> x1, Pallas kernels: none -> 55 us  [on_device(): pl.pallas_call(functools.partial(kernel, S, HD), out_shape=(jax.ShapeDtyp...]
    reduce_scatter x2 -> x0, waiting for transfers between devices: 32 us -> none  [the longest x1 24.8 us: on_device(): lax.psum_scatter(grad_c_all.reshape(tok_rows, state_dim), 'head', scatter...]
    unnamed x24 -> x12, local copies, waits for them, and re-layouts: 28.2 us -> 5.45 us
    reduce_sum x8 -> x0, other arithmetic: 20.4 us -> none  [the longest x4 12.8 us: one_block(): head_total = jnp.sum(pair_in, axis=0)]
    another operation x38 -> x0, other arithmetic: 20 us -> none
    all_to_all x0 -> x1, blocking collectives: none -> 19.9 us  [on_device(): lax.all_to_all(ordered, 'seq', split_axis=0, concat_axis=1, tiled=True)]
    dynamic_slice x28 -> x0, local copies, waits for them, and re-layouts: 17 us -> none  [on_device(): lax.scan(one_block, jnp.zeros((), jnp.float32), items)]
  transfers between devices with their start and end apart: 5 -> 1, of which waited for: 4 -> 1; matrix products, arithmetic and copies ran while one was open for 13% -> 1% of each run, Pallas kernels for 0% -> 0%
where the time goes in v1:
time: 98.2 us; the launch traced here: 97.9 us
  Pallas kernels  55 us (56%)
  blocking collectives  19.9 us (20%)
  local copies, waits for them, and re-layouts  9.32 us (9%)
  waiting for transfers between devices  6.85 us (7%)
  starting transfers between devices  5.23 us (5%)
    pallas_call x1, Pallas kernels, on_device(): pl.pallas_call(functools.partial(kernel, S, HD), out_shape=(jax.ShapeDtyp...  55 us
    all_to_all x1, blocking collectives, on_device(): lax.all_to_all(ordered, 'seq', split_axis=0, concat_axis=1, tiled=True)  19.9 us
    all_to_all x1, waiting for transfers between devices, on_device(): lax.all_to_all(lax.all_to_all(ordered, 'seq', split_axis=0, concat_axis=1...  6.85 us
    unnamed x12, local copies, waits for them, and re-layouts  5.45 us
    all_to_all x1, starting transfers between devices, on_device(): lax.all_to_all(lax.all_to_all(ordered, 'seq', split_axis=0, concat_axis=1...  5.23 us
  transfers between devices with their start and end apart: 1, of which 1 were waited for; matrix products, arithmetic and copies ran while one was open for 1% of the time, Pallas kernels for 0%

profile of v1, /device:TPU:1, one launch (start us, length us, event | category | flops | bytes accessed | tf_op | source)
XLA Modules:
  0.0 97.9 jit_solution(9033202502685545079)
XLA Ops:
  0.6 0.0 copy-start
  0.6 0.7 compare_select_fusion.1
  1.4 0.6 scatter_custom_fusion
  2.0 0.0 copy-done
  2.0 0.0 copy-start.3
  2.0 0.6 gather_fusion
  2.6 0.1 broadcast_select_fusion
  2.7 19.9 %all_to_all.27 = f32[8,8,16,128]{3,2,1,0:T(8,128)} all-to-all(f32[8,8,16,128]{3,2,1,0:T(8,128)S(1)} %broadcast_select_fusion), channel_id=1, replica_groups=mesh['seq'=8,'head'=4] {'seq'}, dimensions={0} | all-to-all | bytes 1048576 | tf_op jit(solution)/shard_map/all_to_all | solution.py:426
  22.7 5.2 %all-to-all-start.1 = ((f32[1,64,16,128]{3,2,0,1:T(8,128)}), f32[1,64,16,128]{3,2,0,1:T(8,128)S(1)}, u32[]{:S(2)}, u32[]{:S(2)}) async-start(f32[1,64,16,128]{3,2,0,1:T(8,128)} %bitcast.3), calls=%async_computation.1 | async-start | bytes 1048576 | tf_op jit(solution)/shard_map/all_to_all | solution.py:425
  27.9 0.0 copy-done.3
  27.9 1.0 %copy.20.raw_ref = f32[1024,16]{1,0:T(8,128)} copy(f32[1024,16]{0,1:T(8,128)S(1)} %copy-done.3) | data formatting | bytes 131072 | tf_op args[4]
  28.9 6.8 %all-to-all-done.1 = f32[1,64,16,128]{3,2,0,1:T(8,128)S(1)} async-done(((f32[1,64,16,128]{3,2,0,1:T(8,128)}), f32[1,64,16,128]{3,2,0,1:T(8,128)S(1)}, u32[]{:S(2)}, u32[]{:S(2)}) %all-to-all-start.1) | async-done | bytes 524320 | tf_op jit(solution)/shard_map/all_to_all | solution.py:425
  35.7 0.8 copy.19
  36.6 55.0 %ssm_backward.1 = (bf16[1024,1024]{1,0:T(8,128)(2,1)}, f32[1024,16]{1,0:T(8,128)}, f32[256,128]{1,0:T(8,128)}, f32[256,128]{1,0:T(8,128)}) custom-call(bf16[1024,1024]{1,0:T(8,128)(2,1)} %x_ref.1, bf16[1024,1024]{1,0:T(8,128)(2,1)} %dy_ref.1, bf16[1024,128]{1,0:T(8,128)(2,1)} %b_ref.1, bf16[1024,128]{1,0:T(8,128)(2,1)} %c_ref.1, f32[1024,16]{1,0:T(8,128)} %copy.20.raw_ref, ...), custom_call_target="tpu_custom_call" | custom-call | tf_op jit(solution)/shard_map/ssm_backward/pallas_call | solution.py:435
  91.6 1.8 %copy.21 = f32[1024,16]{0,1:T(8,128)} copy(f32[1024,16]{1,0:T(8,128)} %get-tuple-element.13) | data formatting | bytes 131072 | tf_op jit(solution)/shard_map/ssm_backward/pallas_call | solution.py:435
  93.4 0.0 copy-start.2
  93.4 0.0 copy-start.1
  93.4 3.1 %copy.25 = bf16[1024,1024]{1,0:T(8,128)(2,1)} copy(bf16[1024,1024]{1,0:T(8,128)(2,1)} %get-tuple-element.20) | data formatting | bytes 4194304
  96.5 0.0 copy-done.2
  96.5 0.7 copy.26
  97.2 0.0 copy-done.1
  97.2 0.7 copy.27
  (4 shorter events, 0.0 us)
Async XLA Ops:
  0.6 1.4 %copy-start = (f32[8,8,16,128]{3,2,1,0:T(8,128)S(1)}, f32[8,8,16,128]{3,2,1,0:T(8,128)}, u32[]{:S(2)}) copy-start(f32[8,8,16,128]{3,2,1,0:T(8,128)} %param.18) | copy-start | bytes 1572868
  2.0 25.9 %copy-start.3 = (f32[1024,16]{0,1:T(8,128)S(1)}, f32[1024,16]{0,1:T(8,128)}, u32[]{:S(2)}) copy-start(f32[1024,16]{0,1:T(8,128)} %param.14) | copy-start | bytes 196612
  22.7 13.1 %all-to-all-start.1 = ((f32[1,64,16,128]{3,2,0,1:T(8,128)}), f32[1,64,16,128]{3,2,0,1:T(8,128)S(1)}, u32[]{:S(2)}, u32[]{:S(2)}) async-start(f32[1,64,16,128]{3,2,0,1:T(8,128)} %bitcast.3), calls=%async_computation.1 | async-start | bytes 1048576 | tf_op jit(solution)/shard_map/all_to_all | solution.py:425
  93.4 3.1 %copy-start.2 = (f32[256,128]{1,0:T(8,128)S(1)}, f32[256,128]{1,0:T(8,128)}, u32[]{:S(2)}) copy-start(f32[256,128]{1,0:T(8,128)} %get-tuple-element.22) | copy-start | bytes 393220
  93.4 3.8 %copy-start.1 = (f32[256,128]{1,0:T(8,128)S(1)}, f32[256,128]{1,0:T(8,128)}, u32[]{:S(2)}) copy-start(f32[256,128]{1,0:T(8,128)} %get-tuple-element.23) | copy-start | bytes 393220

commit v2 on v1

--- a/solution.py
+++ b/solution.py
@@ -9,6 +9,7 @@
 from jax.sharding import PartitionSpec as P
 
 MESH = pl.DeviceIdType.MESH
+STAGES = 4
 LB = 128
 f32, bf16 = jnp.float32, jnp.bfloat16
 LOG2E = math.log2(math.e)
@@ -243,6 +244,14 @@
         bsend[k] = jnp.where(first, incoming, middle)
         b_copy(k).start()
 
+    def stage(q):
+        ready = zz == Z - 1 - q if q < STAGES - 1 else zz <= Z - STAGES
+
+        @pl.when(ready)
+        def _():
+            for k in range(half):
+                link(k)
+
     masks = [
         (lax.broadcasted_iota(jnp.int32, (1, 128), 1) // width == a).astype(f32).astype(bf16)
         for a in range(per)
@@ -288,7 +297,10 @@
         fpart[c] = mm(jnp.concatenate([bt, bt], axis=1), xs[c])
         return 0
 
-    lax.fori_loop(0, nblk, intra, 0)
+    lax.fori_loop(0, nblk // 2 + 1, intra, 0)
+    stage(0)
+    lax.fori_loop(nblk // 2 + 1, nblk, intra, 0)
+    stage(1)
 
     for j in range(pairs):
         block = start[per * j : per * j + per].reshape(128, nstate)
@@ -312,7 +324,10 @@
         yint[rows, :] = mm2(prod, redm[...])
         return 0
 
-    lax.fori_loop(0, nblk, forward, 0)
+    lax.fori_loop(0, nblk // 2, forward, 0)
+    stage(2)
+    lax.fori_loop(nblk // 2, nblk, forward, 0)
+    stage(3)
 
     def send_out(acc, recv, ssem, rsem, d):
         to = lax.rem(hd + d, HD)
@@ -327,9 +342,6 @@
 
     for d in range(1, HD):
         send_out(gcacc, gcrecv, gc_send, gc_recv, d).start()
-
-    for k in range(half):
-        link(k)
 
     hi = skip_ref[...].astype(bf16)
     rem1 = skip_ref[...] - hi.astype(f32)

time: 98.2 us -> 89.6 us (0.912)
  Pallas kernels: 55 us -> 46.4 us
    pallas_call x1, Pallas kernels: 55 us -> 46.4 us  [on_device(): pl.pallas_call(functools.partial(kernel, S, HD), out_shape=(jax.ShapeDtyp...]
where the time goes in v2:
time: 89.6 us; the launch traced here: 89.3 us
  Pallas kernels  46.4 us (52%)
  blocking collectives  19.9 us (22%)
  local copies, waits for them, and re-layouts  9.32 us (10%)
  waiting for transfers between devices  6.85 us (8%)
  starting transfers between devices  5.23 us (6%)
    pallas_call x1, Pallas kernels, on_device(): pl.pallas_call(functools.partial(kernel, S, HD), out_shape=(jax.ShapeDtyp...  46.4 us
    all_to_all x1, blocking collectives, on_device(): lax.all_to_all(ordered, 'seq', split_axis=0, concat_axis=1, tiled=True)  19.9 us
    all_to_all x1, waiting for transfers between devices, on_device(): lax.all_to_all(lax.all_to_all(ordered, 'seq', split_axis=0, concat_axis=1...  6.85 us
    unnamed x12, local copies, waits for them, and re-layouts  5.45 us
    all_to_all x1, starting transfers between devices, on_device(): lax.all_to_all(lax.all_to_all(ordered, 'seq', split_axis=0, concat_axis=1...  5.23 us
    pallas_call x1, local copies, waits for them, and re-layouts, on_device(): pl.pallas_call(functools.partial(kernel, S, HD), out_shape=(jax.ShapeDtyp...  1.84 us
  transfers between devices with their start and end apart: 1, of which 1 were waited for; matrix products, arithmetic and copies ran while one was open for 1% of the time, Pallas kernels for 0%

profile of v2, /device:TPU:1, one launch (start us, length us, event | category | flops | bytes accessed | tf_op | source)
XLA Modules:
  0.0 89.3 jit_solution(16679832269497406351)
XLA Ops:
  0.6 0.0 copy-start
  0.6 0.7 compare_select_fusion.1
  1.4 0.6 scatter_custom_fusion
  2.0 0.0 copy-done
  2.0 0.0 copy-start.3
  2.0 0.6 gather_fusion
  2.6 0.1 broadcast_select_fusion
  2.7 19.9 %all_to_all.27 = f32[8,8,16,128]{3,2,1,0:T(8,128)} all-to-all(f32[8,8,16,128]{3,2,1,0:T(8,128)S(1)} %broadcast_select_fusion), channel_id=1, replica_groups=mesh['seq'=8,'head'=4] {'seq'}, dimensions={0} | all-to-all | bytes 1048576 | tf_op jit(solution)/shard_map/all_to_all | solution.py:438
  22.7 5.2 %all-to-all-start.1 = ((f32[1,64,16,128]{3,2,0,1:T(8,128)}), f32[1,64,16,128]{3,2,0,1:T(8,128)S(1)}, u32[]{:S(2)}, u32[]{:S(2)}) async-start(f32[1,64,16,128]{3,2,0,1:T(8,128)} %bitcast.3), calls=%async_computation.1 | async-start | bytes 1048576 | tf_op jit(solution)/shard_map/all_to_all | solution.py:437
  27.9 0.0 copy-done.3
  27.9 1.0 %copy.20.raw_ref = f32[1024,16]{1,0:T(8,128)} copy(f32[1024,16]{0,1:T(8,128)S(1)} %copy-done.3) | data formatting | bytes 131072 | tf_op args[4]
  28.9 6.8 %all-to-all-done.1 = f32[1,64,16,128]{3,2,0,1:T(8,128)S(1)} async-done(((f32[1,64,16,128]{3,2,0,1:T(8,128)}), f32[1,64,16,128]{3,2,0,1:T(8,128)S(1)}, u32[]{:S(2)}, u32[]{:S(2)}) %all-to-all-start.1) | async-done | bytes 524320 | tf_op jit(solution)/shard_map/all_to_all | solution.py:437
  35.7 0.8 copy.19
  36.6 46.4 %ssm_backward.1 = (bf16[1024,1024]{1,0:T(8,128)(2,1)}, f32[1024,16]{1,0:T(8,128)}, f32[256,128]{1,0:T(8,128)}, f32[256,128]{1,0:T(8,128)}) custom-call(bf16[1024,1024]{1,0:T(8,128)(2,1)} %x_ref.1, bf16[1024,1024]{1,0:T(8,128)(2,1)} %dy_ref.1, bf16[1024,128]{1,0:T(8,128)(2,1)} %b_ref.1, bf16[1024,128]{1,0:T(8,128)(2,1)} %c_ref.1, f32[1024,16]{1,0:T(8,128)} %copy.20.raw_ref, ...), custom_call_target="tpu_custom_call" | custom-call | tf_op jit(solution)/shard_map/ssm_backward/pallas_call | solution.py:447
  83.1 1.8 %copy.21 = f32[1024,16]{0,1:T(8,128)} copy(f32[1024,16]{1,0:T(8,128)} %get-tuple-element.13) | data formatting | bytes 131072 | tf_op jit(solution)/shard_map/ssm_backward/pallas_call | solution.py:447
  84.9 0.0 copy-start.2
  84.9 0.0 copy-start.1
  84.9 3.1 %copy.25 = bf16[1024,1024]{1,0:T(8,128)(2,1)} copy(bf16[1024,1024]{1,0:T(8,128)(2,1)} %get-tuple-element.20) | data formatting | bytes 4194304
  88.0 0.0 copy-done.2
  88.0 0.7 copy.26
  88.7 0.0 copy-done.1
  88.7 0.7 copy.27
  (4 shorter events, 0.0 us)
Async XLA Ops:
  0.6 1.4 %copy-start = (f32[8,8,16,128]{3,2,1,0:T(8,128)S(1)}, f32[8,8,16,128]{3,2,1,0:T(8,128)}, u32[]{:S(2)}) copy-start(f32[8,8,16,128]{3,2,1,0:T(8,128)} %param.18) | copy-start | bytes 1572868
  2.0 25.9 %copy-start.3 = (f32[1024,16]{0,1:T(8,128)S(1)}, f32[1024,16]{0,1:T(8,128)}, u32[]{:S(2)}) copy-start(f32[1024,16]{0,1:T(8,128)} %param.14) | copy-start | bytes 196612
  22.7 13.1 %all-to-all-start.1 = ((f32[1,64,16,128]{3,2,0,1:T(8,128)}), f32[1,64,16,128]{3,2,0,1:T(8,128)S(1)}, u32[]{:S(2)}, u32[]{:S(2)}) async-start(f32[1,64,16,128]{3,2,0,1:T(8,128)} %bitcast.3), calls=%async_computation.1 | async-start | bytes 1048576 | tf_op jit(solution)/shard_map/all_to_all | solution.py:437
  84.9 3.1 %copy-start.2 = (f32[256,128]{1,0:T(8,128)S(1)}, f32[256,128]{1,0:T(8,128)}, u32[]{:S(2)}) copy-start(f32[256,128]{1,0:T(8,128)} %get-tuple-element.22) | copy-start | bytes 393220
  84.9 3.8 %copy-start.1 = (f32[256,128]{1,0:T(8,128)S(1)}, f32[256,128]{1,0:T(8,128)}, u32[]{:S(2)}) copy-start(f32[256,128]{1,0:T(8,128)} %get-tuple-element.23) | copy-start | bytes 393220
